TPU v7x, 8 devices: a whole 2x2x1 slice. The times are simulated.
8 devices in a mesh: dp: 2 (over z, y), ep: 4 (over x, core).
Axes of the slice: x: 2, y: 2, z: 1, core: 2. Of those that a mesh axis runs over, the one named last changes fastest.
Arguments:
- hidden: bfloat16 [8192, 2048], P(('dp', 'ep')), parts along dimension 0
- expert_ids: int32 [8192, 2], P(('dp', 'ep')), parts along dimension 0
- norm_gain: bfloat16 [2048], replicated
- w_router: bfloat16 [2048, 8], replicated
- w_gate: bfloat16 [8, 2048, 5632], P('ep')
- w_up: bfloat16 [8, 2048, 5632], P('ep')
- w_down: bfloat16 [8, 5632, 2048], P('ep')
Outputs:
- output: bfloat16 [8192, 2048], P(('dp', 'ep')), parts along dimension 0
There are 2 independent parts. A program takes and returns all parts, laid end to end along the dimension named above; an argument that names none is the same for every part.
All inputs are finite; a program needn't handle non-finite values.
Results may differ from a plain program's by a relative error of at most 0.00119.
Values are sent between devices in bfloat16 or wider.
A program may use at most 1 GiB of HBM per device.

v0:
```python
import jax
import jax.numpy as jnp
from jax import lax
from jax.sharding import PartitionSpec as P

NORM_EPS = 1e-5


def rms_norm(hidden, norm_gain):
    hidden_f32 = hidden.astype(jnp.float32)
    mean_sq = jnp.mean(hidden_f32 * hidden_f32, axis=-1, keepdims=True)
    return (hidden_f32 * lax.rsqrt(mean_sq + NORM_EPS) * norm_gain.astype(jnp.float32)).astype(jnp.bfloat16)


def route_gates(normed, expert_ids, w_router):
    logits = jnp.dot(normed, w_router, preferred_element_type=jnp.float32)
    hit_mask = expert_ids[:, :, None] == jnp.arange(w_router.shape[1])[None, None, :]
    picked = jnp.sum(jnp.where(hit_mask, logits[:, None, :], 0.0), axis=-1)
    return jax.nn.softmax(picked, axis=-1)


def slot_positions(expert_ids, experts):
    tok_rows = expert_ids.shape[0]
    slot_order = jnp.concatenate([expert_ids[:, 0], expert_ids[:, 1]])
    hit_table = (slot_order[:, None] == jnp.arange(experts)[None, :]).astype(jnp.int32)
    seen_before = jnp.cumsum(hit_table, axis=0) - hit_table
    slot_rank = jnp.sum(seen_before * hit_table, axis=1)
    return slot_rank.reshape(2, tok_rows).T


def solution(mesh):
    token_spec = P(("dp", "ep"), None)
    expert_spec = P("ep", None, None)

    def local_block(hidden, expert_ids, norm_gain, w_router, w_gate, w_up, w_down):
        tok_rows, model_width = hidden.shape
        experts = w_router.shape[1]
        local_experts = w_gate.shape[0]
        group_size = experts // local_experts
        capacity = (5 * tok_rows + 2 * experts - 1) // (2 * experts)
        normed = rms_norm(hidden, norm_gain)
        gate_probs = route_gates(normed, expert_ids, w_router)
        positions = slot_positions(expert_ids, experts)
        expert_grid = jnp.arange(group_size)[None, :] * local_experts + jnp.arange(local_experts)[:, None]
        select = ((expert_ids[:, :, None, None, None] == expert_grid[:, :, None])
                  & (positions[:, :, None, None, None] == jnp.arange(capacity))).astype(jnp.bfloat16)
        send_buf = jnp.einsum("tslgc,td->lgcd", select, normed, preferred_element_type=jnp.float32).astype(jnp.bfloat16)
        send_buf = send_buf.reshape(local_experts, group_size * capacity, model_width)
        recv_buf = lax.all_to_all(send_buf, "ep", 1, 1, tiled=True)
        gate_proj = jnp.einsum("emd,edf->emf", recv_buf, w_gate, preferred_element_type=jnp.float32)
        up_proj = jnp.einsum("emd,edf->emf", recv_buf, w_up, preferred_element_type=jnp.float32)
        hidden_act = (jax.nn.silu(gate_proj) * up_proj).astype(jnp.bfloat16)
        expert_out = jnp.einsum("emf,efd->emd", hidden_act, w_down, preferred_element_type=jnp.float32).astype(jnp.bfloat16)
        back_buf = lax.all_to_all(expert_out, "ep", 1, 1, tiled=True)
        back_buf = back_buf.reshape(local_experts, group_size, capacity, model_width)
        fetched = jnp.einsum("tslgc,lgcd->tsd", select, back_buf, preferred_element_type=jnp.float32)
        mixed_sum = jnp.sum(gate_probs[:, :, None] * fetched, axis=1)
        return (hidden.astype(jnp.float32) + mixed_sum).astype(jnp.bfloat16)

    return jax.shard_map(local_block, mesh=mesh,
                         in_specs=(token_spec, token_spec, P(None), P(None, None), expert_spec, expert_spec, expert_spec),
                         out_specs=token_spec, check_vma=False)
```

profile of v0, /device:TPU:0, one launch (start us, length us, event | category | flops | bytes accessed | tf_op | source)
XLA Modules:
  0.0 658.0 jit_solution(4274168668941181281)
XLA Ops:
  0.0 0.1 iota_add_fusion
  0.1 3.1 fusion.12
  3.2 0.7 convert_element_type.36
  3.9 0.8 fusion.33
  4.7 0.8 broadcast_compare_fusion
  5.5 2.3 reduce-window.6
  7.8 0.3 slice_reduce_fusion
  8.1 0.2 reduce-window.9
  8.2 0.1 add_bitcast_fusion
  8.4 0.3 iota_compare_fusion
  8.8 0.8 copy-done.2
  9.6 3.1 convert_reduce_fusion
  12.7 13.3 %fusion.20 = bf16[2,4,320,2048]{3,2,1,0:T(8,128)(2,1)S(1)} fusion(bf16[1024,2,4,320]{0,3,1,2:T(8,128)(2,1)S(1)} %convert_reduce_fusion, bf16[1024,2048]{1,0:T(8,128)(2,1)} %param.7, f32[2048]{0:T(1024)S(1)} %convert_element_type.36, f32[1024]{0:T(1024)S(1)} %add_rsqrt_fusion), kind=kOutput, calls=%fused_computation.24 | convolution fusion | flops 10745806848 | bytes 19935232 | tf_op jit(solution)/shard_map/tslgc,td->lgcd/dot_general | solution.py:47
  26.0 21.6 %copy.33 = bf16[2,1280,2048]{2,0,1:T(2,128)(2,1)S(1)} copy(bf16[2,1280,2048]{2,1,0:T(8,128)(2,1)S(1)} %bitcast.51) | data formatting | bytes 20971520 | tf_op jit(solution)/shard_map/reshape | solution.py:48
  47.6 120.6 %all_to_all.10 = bf16[2,1280,2048]{2,0,1:T(2,128)(2,1)} all-to-all(bf16[2,1280,2048]{2,0,1:T(2,128)(2,1)S(1)} %copy.33), channel_id=1, replica_groups=mesh['dp'=2,'ep'=4] {'ep'}, dimensions={1} | all-to-all | bytes 20971520 | tf_op jit(solution)/shard_map/all_to_all | solution.py:49
  168.2 118.3 %fusion.10 = f32[2,1280,5632]{2,1,0:T(8,128)} fusion(bf16[2,2048,5632]{2,1,0:T(8,128)(2,1)} %param.11, bf16[2,1280,2048]{2,0,1:T(2,128)(2,1)} %all_to_all.10), kind=kOutput, calls=%fused_computation.18 | convolution fusion | flops 59055800320 | bytes 114294784 | tf_op jit(solution)/shard_map/emd,edf->emf/dot_general | solution.py:50
  286.5 122.7 %multiply_convert_fusion = bf16[2,1280,5632]{2,1,0:T(8,128)(2,1)} fusion(f32[2,1280,5632]{2,1,0:T(8,128)} %fusion.10, bf16[2,2048,5632]{2,1,0:T(8,128)(2,1)} %param.12, bf16[2,1280,2048]{2,0,1:T(2,128)(2,1)} %all_to_all.10), kind=kOutput, calls=%fused_computation | convolution fusion | flops 59142307840 | bytes 143130624 | tf_op jit(solution)/shard_map/emd,edf->emf/dot_general | solution.py:51
  409.2 69.3 %convolution_convert_fusion = bf16[2,1280,2048]{2,1,0:T(8,128)(2,1)} fusion(bf16[2,1280,5632]{2,1,0:T(8,128)(2,1)} %multiply_convert_fusion, bf16[2,5632,2048]{2,1,0:T(8,128)(2,1)} %param.13), kind=kOutput, calls=%fused_computation.10 | convolution fusion | flops 59061043200 | bytes 85458944 | tf_op jit(solution)/shard_map/emf,efd->emd/dot_general | solution.py:53
  478.5 20.0 %copy.36 = bf16[2,1280,2048]{2,0,1:T(2,128)(2,1)} copy(bf16[2,1280,2048]{2,1,0:T(8,128)(2,1)} %convolution_convert_fusion) | data formatting | bytes 20971520 | tf_op jit(solution)/shard_map/convert_element_type | solution.py:53
  498.5 6.0 all-to-all-start.1
  504.6 3.5 fusion.25
  508.2 111.6 %all-to-all-done.1 = bf16[2,1280,2048]{2,0,1:T(2,128)(2,1)} async-done(((bf16[2,1280,2048]{2,0,1:T(2,128)(2,1)}), bf16[2,1280,2048]{2,0,1:T(2,128)(2,1)}, u32[]{:S(2)}, u32[]{:S(2)}) %all-to-all-start.1) | async-done | bytes 10485792 | tf_op jit(solution)/shard_map/all_to_all | solution.py:54
  619.8 30.9 %fusion.2 = f32[1024,2048]{1,0:T(8,128)} fusion(f32[1024,2]{0,1:T(2,128)S(1)} %fusion.31, bf16[2,4,320,2048,1]{3,0,2,1,4:T(2,128)(2,1)} %bitcast.10, pred[1024,2,320]{0,2,1:T(8,128)(4,1)S(1)} %copy-done.3, pred[1024,2,2,4]{0,2,3,1:T(4,128)(4,1)S(1)} %copy-done.5), kind=kOutput, calls=%fused_computation.6 | convolution fusion | flops 21486370816 | bytes 19554304 | tf_op jit(solution)/shard_map/tslgc,lgcd->tsd/dot_general | solution.py:56
  650.7 7.1 %fusion.15 = bf16[1024,2048]{1,0:T(8,128)(2,1)} fusion(f32[1024,2048]{1,0:T(8,128)} %fusion.2, bf16[1024,2048]{1,0:T(8,128)(2,1)S(1)} %copy-done.1), kind=kLoop, calls=%fused_computation.23 | loop fusion | flops 6291456 | bytes 16777216 | tf_op jit(solution)/shard_map/convert_element_type | solution.py:58
  (32 shorter events, 0.2 us)
Async XLA Ops:
  0.0 504.5 %copy-start = (bf16[2048,8]{0,1:T(8,128)(2,1)S(1)}, bf16[2048,8]{0,1:T(8,128)(2,1)}, u32[]{:S(2)}) copy-start(bf16[2048,8]{0,1:T(8,128)(2,1)} %param.10) | copy-start | bytes 98308
  3.2 22.8 %copy-start.9 = (f32[1024]{0:T(1024)}, f32[1024]{0:T(1024)S(1)}, u32[]{:S(2)}) copy-start(f32[1024]{0:T(1024)S(1)} %add_rsqrt_fusion) | copy-start | bytes 12292
  3.9 22.1 %copy-start.7 = (f32[2048]{0:T(1024)}, f32[2048]{0:T(1024)S(1)}, u32[]{:S(2)}) copy-start(f32[2048]{0:T(1024)S(1)} %convert_element_type.36) | copy-start | bytes 24580
  5.5 20.5 %copy-start.4 = (pred[1024,2,2,4]{0,2,3,1:T(4,128)(4,1)}, pred[1024,2,2,4]{0,2,3,1:T(4,128)(4,1)S(1)}, u32[]{:S(2)}) copy-start(pred[1024,2,2,4]{0,2,3,1:T(4,128)(4,1)S(1)} %broadcast_compare_fusion) | copy-start | bytes 49156
  8.8 0.8 copy-start.2
  498.5 6.0 copy-start.8
  498.5 6.0 copy-start.10
  498.5 121.3 %all-to-all-start.1 = ((bf16[2,1280,2048]{2,0,1:T(2,128)(2,1)}), bf16[2,1280,2048]{2,0,1:T(2,128)(2,1)}, u32[]{:S(2)}, u32[]{:S(2)}) async-start(bf16[2,1280,2048]{2,0,1:T(2,128)(2,1)} %copy.36), calls=%async_computation.1 | async-start | bytes 20971520 | tf_op jit(solution)/shard_map/all_to_all | solution.py:54
  504.6 3.5 copy-start.6
  504.6 115.3 %copy-start.3 = (pred[1024,2,320]{0,2,1:T(8,128)(4,1)S(1)}, pred[1024,2,320]{0,2,1:T(8,128)(4,1)}, u32[]{:S(2)}) copy-start(pred[1024,2,320]{0,2,1:T(8,128)(4,1)} %copy-done.2) | copy-start | bytes 1966084
  504.6 115.2 %copy-start.5 = (pred[1024,2,2,4]{0,2,3,1:T(4,128)(4,1)S(1)}, pred[1024,2,2,4]{0,2,3,1:T(4,128)(4,1)}, u32[]{:S(2)}) copy-start(pred[1024,2,2,4]{0,2,3,1:T(4,128)(4,1)} %copy-done.4) | copy-start | bytes 49156
  619.8 30.9 %copy-start.1 = (bf16[1024,2048]{1,0:T(8,128)(2,1)S(1)}, bf16[1024,2048]{1,0:T(8,128)(2,1)}, u32[]{:S(2)}) copy-start(bf16[1024,2048]{1,0:T(8,128)(2,1)} %param.7) | copy-start | bytes 12582916
where the time goes:
time: 666 us; the launch traced here: 658 us
  matrix products  358 us (54%)
  blocking collectives  121 us (18%)
  waiting for transfers between devices  112 us (17%)
  local copies, waits for them, and re-layouts  43.6 us (7%)
  other arithmetic  17.9 us (3%)
    dot_general x1, matrix products, local_block(): jnp.einsum('emd,edf->emf', recv_buf, w_up, preferred_element_type=jnp.flo...  123 us
    all_to_all x1, blocking collectives, local_block(): recv_buf = lax.all_to_all(send_buf, 'ep', 1, 1, tiled=True)  121 us
    dot_general x1, matrix products, local_block(): jnp.einsum('emd,edf->emf', recv_buf, w_gate, preferred_element_type=jnp.f...  118 us
    all_to_all x1, waiting for transfers between devices, local_block(): back_buf = lax.all_to_all(expert_out, 'ep', 1, 1, tiled=True)  112 us
    dot_general x1, matrix products, local_block(): jnp.einsum('emf,efd->emd', hidden_act, w_down, preferred_element_type=jnp...  69.3 us
    dot_general x1, matrix products, local_block(): jnp.einsum('tslgc,lgcd->tsd', select, back_buf, preferred_element_type=jn...  30.9 us
    reshape x1, local copies, waits for them, and re-layouts, local_block(): send_buf.reshape(local_experts, group_size * capacity, model_width)  21.6 us
    convert_element_type x1, local copies, waits for them, and re-layouts, local_block(): jnp.einsum('emf,efd->emd', hidden_act, w_down, preferred_element_type=jnp...  20 us
  transfers between devices with their start and end apart: 1, of which 1 were waited for; matrix products, arithmetic and copies ran while one was open for 1% of the time, Pallas kernels for 0%

commit v1 on v0

v1 whole, which is shorter than its diff:
```python
import functools

import jax
import jax.numpy as jnp
from jax import lax
from jax.experimental import pallas as pl
from jax.experimental.pallas import tpu as pltpu
from jax.sharding import PartitionSpec as P


NORM_EPS = 1e-5
F32 = jnp.float32
BF16 = jnp.bfloat16
BLK = 16
NBUF = 3
TF = 512
ANY = pl.BlockSpec(memory_space=pl.ANY)
SMEM = pl.BlockSpec(memory_space=pltpu.SMEM)
VMEM = pl.BlockSpec(memory_space=pltpu.VMEM)
MIB = 2**20


def up_to(n, m):
    return (n + m - 1) // m * m


def pack_rows(normed, queue, expert, cap):
    place = queue[pl.ds(expert, 1), :]
    rows = lax.broadcasted_iota(jnp.int32, (cap, place.shape[1]), 0)
    pick = (rows == place).astype(F32).astype(BF16)
    return jnp.dot(pick, normed, preferred_element_type=F32).astype(BF16)


def route_kernel(cap, exps, hid, ids, idst, gain, w_router, normed, queue, codes, gates, counts, *far0):
    tok, _ = hid.shape
    experts = w_router.shape[1]
    step = 256
    for i in range(0, tok, step):
        x = hid[i:i + step, :].astype(F32)
        mean_sq = jnp.mean(x * x, axis=-1, keepdims=True)
        normed[i:i + step, :] = (x * lax.rsqrt(mean_sq + NORM_EPS) * gain[...].astype(F32)).astype(BF16)

    eye_t = lax.broadcasted_iota(jnp.int32, (experts, tok), 0)
    hit0_t = (idst[0:1, :] == eye_t).astype(F32)
    hit1_t = (idst[1:2, :] == eye_t).astype(F32)
    tot0_t = jnp.sum(hit0_t, axis=1, keepdims=True)
    tot1_t = jnp.sum(hit1_t, axis=1, keepdims=True)
    both_t = jnp.concatenate([hit0_t, hit1_t], axis=0).astype(BF16)
    for i in range(0, tok, step):
        before = (lax.broadcasted_iota(jnp.int32, (tok, step), 0)
                  < i + lax.broadcasted_iota(jnp.int32, (tok, step), 1)).astype(F32).astype(BF16)
        seen = jnp.dot(both_t, before, preferred_element_type=F32)
        h0, h1 = hit0_t[:, i:i + step], hit1_t[:, i:i + step]
        place = jnp.where(h0 > 0, seen[:experts], jnp.where(h1 > 0, seen[experts:] + tot0_t, -1.0))
        queue[:, i:i + step] = place.astype(jnp.int32)
    counts[...] = jnp.broadcast_to(jnp.minimum(tot0_t + tot1_t, float(cap)), counts.shape).astype(jnp.int32)

    eye = lax.broadcasted_iota(jnp.int32, (tok, experts), 1)
    hit0 = (ids[:, 0:1] == eye).astype(F32)
    hit1 = (ids[:, 1:2] == eye).astype(F32)
    tot0 = jnp.sum(hit0, axis=0, keepdims=True)
    both = jnp.concatenate([hit0, hit1], axis=1).astype(BF16)
    for i in range(0, tok, step):
        before = (i + lax.broadcasted_iota(jnp.int32, (step, tok), 0)
                  > lax.broadcasted_iota(jnp.int32, (step, tok), 1)).astype(F32).astype(BF16)
        seen = jnp.dot(before, both, preferred_element_type=F32)
        h0, h1 = hit0[i:i + step], hit1[i:i + step]
        logits = jnp.dot(normed[i:i + step, :], w_router[...], preferred_element_type=F32)
        pos0 = jnp.sum(h0 * seen[:, :experts], axis=1, keepdims=True).astype(jnp.int32)
        pos1 = jnp.sum(h1 * (seen[:, experts:] + tot0), axis=1, keepdims=True).astype(jnp.int32)
        code0 = jnp.where(pos0 < cap, ids[i:i + step, 0:1] * cap + pos0, -1)
        code1 = jnp.where(pos1 < cap, ids[i:i + step, 1:2] * cap + pos1, -1)
        l0 = jnp.sum(h0 * logits, axis=1, keepdims=True)
        l1 = jnp.sum(h1 * logits, axis=1, keepdims=True)
        top = jnp.maximum(l0, l1)
        e0, e1 = jnp.exp(l0 - top), jnp.exp(l1 - top)
        codes[i:i + step, 0:1] = code0
        codes[i:i + step, 1:2] = code1
        gates[i:i + step, 0:1] = e0 / (e0 + e1)
        gates[i:i + step, 1:2] = e1 / (e0 + e1)

    for k in range(2):
        far0[k][...] = pack_rows(normed[...], queue, exps[k], cap)


def route(exps, hidden, ids, gain, w_router, cap):
    tok, width = hidden.shape
    experts = w_router.shape[1]
    one = jax.ShapeDtypeStruct((cap, width), BF16)
    return pl.pallas_call(
        functools.partial(route_kernel, cap),
        out_shape=[jax.ShapeDtypeStruct((tok, width), BF16), jax.ShapeDtypeStruct((experts, tok), jnp.int32),
                   jax.ShapeDtypeStruct((tok, 2), jnp.int32), jax.ShapeDtypeStruct((tok, 2), F32),
                   jax.ShapeDtypeStruct((experts, 128), jnp.int32), one, one],
        in_specs=[SMEM] + [VMEM] * 5,
        out_specs=[VMEM] * 7,
        cost_estimate=pl.CostEstimate(flops=10**10, bytes_accessed=2 * 10**7, transcendentals=0),
        compiler_params=pltpu.CompilerParams(vmem_limit_bytes=48 * MIB),
    )(exps, hidden, ids, ids.T, gain.reshape(1, width), w_router)


def pack_kernel(cap, exps, normed, queue, *outs):
    for k, out in enumerate(outs):
        out[...] = pack_rows(normed[...], queue, exps[k], cap)


def pack(exps, normed, queue, cap):
    _, width = normed.shape
    one = jax.ShapeDtypeStruct((cap, width), BF16)
    return pl.pallas_call(
        functools.partial(pack_kernel, cap),
        out_shape=[one] * exps.shape[0],
        in_specs=[SMEM] + [VMEM] * 2,
        out_specs=[VMEM] * exps.shape[0],
        cost_estimate=pl.CostEstimate(flops=9 * 10**9, bytes_accessed=2 * 10**7, transcendentals=0),
        compiler_params=pltpu.CompilerParams(vmem_limit_bytes=48 * MIB),
    )(exps, normed, queue)


def ffn_kernel(local, cap, sizes, counts, x0, x1, wg, wu, wd, o0, o1, xs, acc, bg, bu, bd, wsem, sem):
    steps = wg.shape[2] // TF
    n0 = pl.multiple_of((counts[0] + BLK - 1) // BLK * BLK, BLK)
    rows = n0 + counts[1]

    def copies(f, slot):
        cols = pl.ds(pl.multiple_of(f * TF, TF), TF)
        return (pltpu.make_async_copy(wg.at[local, :, cols], bg.at[slot], wsem.at[0, slot]),
                pltpu.make_async_copy(wu.at[local, :, cols], bu.at[slot], wsem.at[1, slot]),
                pltpu.make_async_copy(wd.at[local, cols, :], bd.at[slot], wsem.at[2, slot]))

    def fetch(f, slot):
        for c in copies(f, slot):
            c.start()

    first = pltpu.make_async_copy(x0, xs.at[pl.ds(0, cap)], sem.at[0])
    first.start()
    for s in range(NBUF - 1):
        fetch(s, s)
    acc[...] = jnp.zeros_like(acc)
    first.wait()
    second = pltpu.make_async_copy(x1, xs.at[pl.ds(n0, cap)], sem.at[1])
    second.start()
    second.wait()

    def step(f, _):
        slot = lax.rem(f, NBUF)
        for c in copies(f, slot):
            c.wait()

        @pl.when(f + NBUF - 1 < steps)
        def _():
            fetch(f + NBUF - 1, lax.rem(f + NBUF - 1, NBUF))

        def tile(m):
            x = xs[0:m, :]
            g = jnp.dot(x, bg[slot], preferred_element_type=F32)
            u = jnp.dot(x, bu[slot], preferred_element_type=F32)
            a = (jax.nn.silu(g) * u).astype(BF16)
            acc[0:m, :] += jnp.dot(a, bd[slot], preferred_element_type=F32)

        low = 0
        for m in sizes:
            @pl.when((rows > low) & (rows <= m))
            def _():
                tile(m)

            low = m
        return 0

    lax.fori_loop(0, steps, step, 0)
    xs[...] = acc[...].astype(BF16)
    a = pltpu.make_async_copy(xs.at[pl.ds(0, cap)], o0, sem.at[0])
    b = pltpu.make_async_copy(xs.at[pl.ds(n0, cap)], o1, sem.at[1])
    a.start()
    b.start()
    a.wait()
    b.wait()


def ffn(counts, xs, wg, wu, wd, local, cap):
    width, inner = wg.shape[1:]
    sizes = (2 * cap - 256, 2 * cap - 192, 2 * cap - 128, 2 * cap - 64, 2 * cap)
    return pl.pallas_call(
        functools.partial(ffn_kernel, local, cap, sizes),
        out_shape=[jax.ShapeDtypeStruct(x.shape, BF16) for x in xs],
        in_specs=[SMEM] + [ANY] * (3 + len(xs)),
        out_specs=[ANY] * len(xs),
        scratch_shapes=[pltpu.VMEM((2 * cap, width), BF16), pltpu.VMEM((2 * cap, width), F32),
                        pltpu.VMEM((NBUF, width, TF), BF16), pltpu.VMEM((NBUF, width, TF), BF16),
                        pltpu.VMEM((NBUF, TF, width), BF16),
                        pltpu.SemaphoreType.DMA((3, NBUF)), pltpu.SemaphoreType.DMA((2,))],
        cost_estimate=pl.CostEstimate(flops=6 * 540 * width * inner, bytes_accessed=6 * width * inner, transcendentals=0),
        compiler_params=pltpu.CompilerParams(vmem_limit_bytes=60 * MIB),
    )(counts, *xs, wg, wu, wd)


def merge_kernel(cap, n_buf, final, counts, tgt, codes, gates, base, *refs):
    bufs, out, held = refs[:n_buf], refs[n_buf], refs[n_buf + 1]

    @pl.when(pl.program_id(0) == 0)
    def _():
        at, seg = 0, 0
        for buf in bufs:
            for i in range(0, buf.shape[0], cap):
                live = lax.broadcasted_iota(jnp.int32, (cap, buf.shape[1]), 0) < counts[seg]
                part = buf[i:i + cap, :].astype(F32)
                held[at:at + cap, :] = jnp.where(live, part, 0.0).astype(BF16)
                at, seg = at + cap, seg + 1
        if at < held.shape[0]:
            held[at:, :] = jnp.zeros((held.shape[0] - at, held.shape[1]), BF16)

    got = []
    for s in range(2):
        pick = (codes[:, s:s + 1] == tgt[...]).astype(F32).astype(BF16)
        got.append(gates[:, s:s + 1] * jnp.dot(pick, held[...], preferred_element_type=F32))
    total = got[0] + got[1]
    if base is not None:
        total = base[0][...] + total
    if final:
        total = base[1][...].astype(F32) + total
    out[...] = total.astype(out.dtype)


def merge(experts_of, counts, codes, gates, bufs, cap, partial=None, hidden=None):
    tok, width = codes.shape[0], bufs[0].shape[1]
    deep = up_to(len(experts_of) * cap, 256)
    tgt = (jnp.stack(experts_of)[:, None] * cap + jnp.arange(cap)[None, :]).reshape(1, -1)
    tgt = jnp.pad(tgt, ((0, 0), (0, deep - tgt.shape[1])), constant_values=-2).astype(jnp.int32)
    final = hidden is not None
    rows = 256
    tile = pl.BlockSpec((rows, width), lambda i: (i, 0))
    pair = pl.BlockSpec((rows, 2), lambda i: (i, 0))
    extra = [partial, hidden] if final else []
    n_buf = len(bufs)

    def body(counts, tgt, codes, gates, *refs):
        base = refs[:len(extra)] if extra else None
        merge_kernel(cap, n_buf, final, counts, tgt, codes, gates, base, *refs[len(extra):])

    return pl.pallas_call(
        body,
        out_shape=jax.ShapeDtypeStruct((tok, width), BF16 if final else F32),
        grid=(tok // rows,),
        in_specs=[SMEM, pl.BlockSpec((1, deep), lambda i: (0, 0)), pair, pair] + [tile] * len(extra)
        + [pl.BlockSpec(b.shape, lambda i: (0, 0)) for b in bufs],
        out_specs=tile,
        scratch_shapes=[pltpu.VMEM((deep, width), BF16)],
        cost_estimate=pl.CostEstimate(flops=4 * tok * deep * width, bytes_accessed=2 * 10**7, transcendentals=0),
        compiler_params=pltpu.CompilerParams(vmem_limit_bytes=56 * MIB),
    )(jnp.stack(counts), tgt, codes, gates, *extra, *bufs)


def solution(mesh):
    token_spec = P(("dp", "ep"), None)
    expert_spec = P("ep", None, None)

    def local_block(hidden, expert_ids, norm_gain, w_router, w_gate, w_up, w_down):
        tok, _ = hidden.shape
        experts = w_router.shape[1]
        per = w_gate.shape[0]
        group = experts // per
        cap = (5 * tok + 2 * experts - 1) // (2 * experts)
        me = lax.axis_index("ep")
        peer = [me ^ k for k in range(group)]

        def swap(x, k):
            return lax.ppermute(x, "ep", [(i, i ^ k) for i in range(group)])

        def ids_of(pairs):
            return [per * peer[k] + i for k, i in pairs]

        def after(x, *earlier):
            return lax.optimization_barrier((x, *earlier))[0]

        normed, queue, codes, gates, n_mine, *far0 = route(
            jnp.stack(ids_of([(2, 0), (3, 0)])), hidden, expert_ids, norm_gain, w_router, cap)
        got0 = [swap(far0[0], 2), swap(far0[1], 3)]
        n_all = lax.all_gather(n_mine[:, 0], "ep")
        own0, sib0, own1, sib1, *far1 = pack(
            jnp.stack(ids_of([(0, 0), (1, 0), (0, 1), (1, 1), (2, 1), (3, 1)])), normed, queue, cap)
        sib0, sib1 = swap(sib0, 1), swap(sib1, 1)
        got1 = [swap(far1[0], 2), swap(far1[1], 3)]

        def run(i, k, xs, *earlier):
            expert = per * me + i
            counts = jnp.stack([n_all[peer[k], expert], n_all[peer[k + 1], expert]])
            return ffn(after(counts, *earlier), xs, w_gate, w_up, w_down, i, cap)

        o_own0, o_sib0 = run(0, 0, [own0, sib0])
        o_far0 = run(0, 2, got0, o_own0)
        back0 = [swap(o_far0[0], 2), swap(o_far0[1], 3)]
        o_far1 = run(1, 2, got1, o_far0[0])
        back1 = [swap(o_far1[0], 2), swap(o_far1[1], 3)]
        o_own1, o_sib1 = run(1, 0, [own1, sib1], o_far1[0])
        back_sib = [swap(o_sib0, 1), swap(o_sib1, 1)]

        def gather(pairs, bufs, **kw):
            experts_of = ids_of(pairs)
            return merge(experts_of, [n_all[me, e] for e in experts_of], codes, gates, bufs, cap, **kw)

        partial = gather([(0, 0), (1, 0), (0, 1), (1, 1), (2, 0), (3, 0)],
                         [o_own0, back_sib[0], o_own1, back_sib[1]] + back0)
        return gather([(2, 1), (3, 1)], back1, partial=partial, hidden=hidden)

    return jax.shard_map(local_block, mesh=mesh,
                         in_specs=(token_spec, token_spec, P(None), P(None, None), expert_spec, expert_spec, expert_spec),
                         out_specs=token_spec, check_vma=False)
```

time: 666 us -> 490 us (0.74)
  matrix products: 358 us -> 0 us
  Pallas kernels: 0 us -> 255 us
  waiting for transfers between devices: 112 us -> 78.8 us
  local copies, waits for them, and re-layouts: 43.6 us -> 17 us
  blocking collectives: 121 us -> 110 us
  other arithmetic: 17.9 us -> 9.67 us
    dot_general x6 -> x0, matrix products: 358 us -> none  [the longest x1 123 us: local_block(): jnp.einsum('emd,edf->emf', recv_buf, w_up, preferred_element_type=jnp.flo...]
    pallas_call x0 -> x8, Pallas kernels: none -> 255 us  [the longest x4 197 us: ffn(): pl.pallas_call(functools.partial(ffn_kernel, local, cap, sizes), out_shap...]
    all_to_all x1 -> x0, blocking collectives: 121 us -> none  [local_block(): recv_buf = lax.all_to_all(send_buf, 'ep', 1, 1, tiled=True)]
    all_to_all x1 -> x0, waiting for transfers between devices: 112 us -> none  [local_block(): back_buf = lax.all_to_all(expert_out, 'ep', 1, 1, tiled=True)]
    unnamed x0 -> x1, blocking collectives: none -> 110 us
    ppermute x0 -> x12, waiting for transfers between devices: none -> 78.8 us  [swap(): return lax.ppermute(x, 'ep', [(i, i ^ k) for i in range(group)])]
    reshape x2 -> x1, local copies, waits for them, and re-layouts: 21.6 us -> 0.7 us  [route(): gain.reshape(1, width)]
    convert_element_type x1 -> x0, local copies, waits for them, and re-layouts: 20 us -> none  [local_block(): jnp.einsum('emf,efd->emd', hidden_act, w_down, preferred_element_type=jnp...]
  transfers between devices with their start and end apart: 1 -> 12, of which waited for: 1 -> 4; matrix products, arithmetic and copies ran while one was open for 1% -> 4% of each run, Pallas kernels for 0% -> 36%
where the time goes in v1:
time: 490 us; the launch traced here: 481 us
  Pallas kernels  255 us (52%)
  blocking collectives  110 us (22%)
  waiting for transfers between devices  78.8 us (16%)
  local copies, waits for them, and re-layouts  17 us (3%)
  other arithmetic  9.67 us (2%)
  starting transfers between devices  9.36 us (2%)
    pallas_call x4, Pallas kernels, ffn(): pl.pallas_call(functools.partial(ffn_kernel, local, cap, sizes), out_shap...  197 us
    unnamed x1, blocking collectives  110 us
    ppermute x12, waiting for transfers between devices, swap(): return lax.ppermute(x, 'ep', [(i, i ^ k) for i in range(group)])  78.8 us
    pallas_call x2, Pallas kernels, merge(): pl.pallas_call(body, out_shape=jax.ShapeDtypeStruct((tok, width), BF16 if...  37.5 us
    pallas_call x1, Pallas kernels, pack(): pl.pallas_call(functools.partial(pack_kernel, cap), out_shape=[one] * exp...  11.6 us
  transfers between devices with their start and end apart: 12, of which 4 were waited for; matrix products, arithmetic and copies ran while one was open for 4% of the time, Pallas kernels for 36%

profile of v1, /device:TPU:0, one launch (start us, length us, event | category | flops | bytes accessed | tf_op | source)
XLA Modules:
  0.0 480.9 jit_solution(15112205173304245712)
XLA Ops:
  3.4 9.3 %shard_map.73 = (bf16[1024,2048]{1,0:T(8,128)(2,1)}, s32[8,1024]{1,0:T(8,128)S(1)}, s32[1024,2]{1,0:T(8,128)S(1)}, f32[1024,2]{1,0:T(8,128)S(1)}, s32[8,128]{1,0...) custom-call(s32[2]{0:T(128)S(1)} %pad_add_fusion.exps, bf16[1024,2048]{1,0:T(8,128)(2,1)} %refs_1_.1, ...), custom_call_target="tpu_custom_call" | custom-call | flops 10000000000 | bytes 20000000 | tf_op jit(solution)/shard_map/pallas_call | solution.py:90
  14.4 11.6 %shard_map.74 = (bf16[320,2048]{1,0:T(8,128)(2,1)S(1)}, bf16[320,2048]{1,0:T(8,128)(2,1)}, bf16[320,2048]{1,0:T(8,128)(2,1)S(1)}, bf16[320,2048]{1,0:T(8,128)(2,...) custom-call(s32[6]{0:T(128)S(1)} %stack.76.exps, bf16[1024,2048]{1,0:T(8,128)(2,1)} %get-tuple-element.32.normed, ...), custom_call_target="tpu_custom_call" | custom-call | flops 8999999488 | bytes 20000000 | tf_op jit(solution)/shard_map/pallas_call | solution.py:110
  26.0 1.1 copy-done
  28.9 2.5 collective-permute-start.2
  31.5 1.7 collective-permute-start.4
  35.4 110.0 %all-reduce.2 = s32[32]{0:T(128)S(1)} all-reduce(s32[32]{0:T(128)S(1)} %dynamic-update-slice), channel_id=2, replica_groups=mesh['dp'=2,'ep'=4] {'ep'}, use_global_device_ids=true, to_apply=%add.2 | all-reduce | flops 32 | bytes 256
  146.2 2.0 pad_add_fusion.2.counts
  148.2 1.8 pad_add_fusion.5.counts
  150.1 1.9 pad_add_fusion.4.counts
  152.0 1.9 pad_add_fusion.3.counts
  153.8 51.1 %shard_map.75 = (bf16[320,2048]{1,0:T(8,128)(2,1)}, bf16[320,2048]{1,0:T(8,128)(2,1)}) custom-call(s32[2]{0:T(128)} %pad_add_fusion.2.counts, bf16[320,2048]{1,0:T(8,128)(2,1)} %copy-done.1, bf16[320,2048]{1,0:T(8,128)(2,1)} %collective-permute-done.x1, bf16[2,2048,5632]{2,1,0:T(8,128)(2,1)} %wg.7, bf16[2,2048,5632]{2,1,0:T(8,128)(2,1)} %wu.7, ...), custom_call_target="tpu_custom_call" | custom-call | flops 37371248640 | bytes 69206016 | tf_op jit(solution)/shard_map/pallas_call | solution.py:183
  205.0 46.9 %shard_map.76 = (bf16[320,2048]{1,0:T(8,128)(2,1)}, bf16[320,2048]{1,0:T(8,128)(2,1)}) custom-call(s32[2]{0:T(128)} %pad_add_fusion.5.counts, bf16[320,2048]{1,0:T(8,128)(2,1)} %collective-permute-done.2.x0, bf16[320,2048]{1,0:T(8,128)(2,1)} %collective-permute-done.3.x1, bf16[2,2048,5632]{2,1,0:T(8,128)(2,1)} %wg.7, bf16[2,2048,5632]{2,1,0:T(8,128)(2,1)} %wu.7, ...), custom_call_target="tpu_custom_call" | custom-call | flops 37371248640 | bytes 69206016 | tf_op jit(solution)/shard_map/pallas_call | solution.py:183
  251.9 51.4 %shard_map.77 = (bf16[320,2048]{1,0:T(8,128)(2,1)}, bf16[320,2048]{1,0:T(8,128)(2,1)}) custom-call(s32[2]{0:T(128)} %pad_add_fusion.4.counts, bf16[320,2048]{1,0:T(8,128)(2,1)} %collective-permute-done.4.x0, bf16[320,2048]{1,0:T(8,128)(2,1)} %collective-permute-done.5.x1, bf16[2,2048,5632]{2,1,0:T(8,128)(2,1)} %wg.7, bf16[2,2048,5632]{2,1,0:T(8,128)(2,1)} %wu.7, ...), custom_call_target="tpu_custom_call" | custom-call | flops 37371248640 | bytes 69206016 | tf_op jit(solution)/shard_map/pallas_call | solution.py:183
  304.3 47.3 %shard_map.78 = (bf16[320,2048]{1,0:T(8,128)(2,1)}, bf16[320,2048]{1,0:T(8,128)(2,1)}) custom-call(s32[2]{0:T(128)} %pad_add_fusion.3.counts, bf16[320,2048]{1,0:T(8,128)(2,1)} %copy-done, bf16[320,2048]{1,0:T(8,128)(2,1)} %copy-done.5, bf16[2,2048,5632]{2,1,0:T(8,128)(2,1)} %wg.7, bf16[2,2048,5632]{2,1,0:T(8,128)(2,1)} %wu.7, bf16[2,5632,2048]{2,1,0:T(8,128)(2,1)} %wd.7), custom_call_target="tpu_custom_call" | custom-call | flops 37371248640 | bytes 69206016 | tf_op jit(solution)/shard_map/pallas_call | solution.py:183
  351.7 1.8 collective-permute-start.9
  355.5 4.5 stack.69.counts
  360.0 1.8 pad_add_fusion.1.counts
  361.9 1.5 collective-permute-start.11
  363.4 20.3 %collective-permute-done.8.refs_4_ = bf16[320,2048]{1,0:T(8,128)(2,1)} collective-permute-done((bf16[320,2048]{1,0:T(8,128)(2,1)}, bf16[320,2048]{1,0:T(8,128)(2,1)}, u32[]{:S(2)}, u32[]{:S(2)}) %collective-permute-start.8) | collective-permute-done | bytes 1310752 | tf_op jit(solution)/shard_map/ppermute | solution.py:267
  383.6 27.1 %collective-permute-done.9.refs_5_ = bf16[320,2048]{1,0:T(8,128)(2,1)} collective-permute-done((bf16[320,2048]{1,0:T(8,128)(2,1)}, bf16[320,2048]{1,0:T(8,128)(2,1)}, u32[]{:S(2)}, u32[]{:S(2)}) %collective-permute-start.9) | collective-permute-done | bytes 1310752 | tf_op jit(solution)/shard_map/ppermute | solution.py:267
  410.7 24.7 %shard_map.79.refs_0_ = f32[1024,2048]{1,0:T(8,128)} custom-call(s32[6]{0:T(128)} %stack.69.counts, s32[1,2048]{1,0:T(1,128)} %pad.9.tgt, s32[1024,2]{1,0:T(8,128)} %copy-done.3, f32[1024,2]{1,0:T(8,128)} %copy-done.4, bf16[320,2048]{1,0:T(8,128)(2,1)} %get-tuple-element.36.refs_0_, bf16[320,2048]{1,0:T(8,128)(2,1)} %collective-permute-done.1.refs_1_, ...), custom_call_target="tpu_custom_call" | custom-call | flops 17179869184 | bytes 20000000 | tf_op jit(solution)/shard_map/pallas_call | solution.py:240
  435.4 4.3 collective-permute-done.10.refs_2_
  439.7 27.1 %collective-permute-done.11.refs_3_ = bf16[320,2048]{1,0:T(8,128)(2,1)S(1)} collective-permute-done((bf16[320,2048]{1,0:T(8,128)(2,1)S(1)}, bf16[320,2048]{1,0:T(8,128)(2,1)S(1)}, u32[]{:S(2)}, u32[]{:S(2)}) %collective-permute-start.11) | collective-permute-done | bytes 1310752 | tf_op jit(solution)/shard_map/ppermute | solution.py:267
  467.9 12.8 %shard_map.80 = bf16[1024,2048]{1,0:T(8,128)(2,1)} custom-call(s32[2]{0:T(128)} %pad_add_fusion.1.counts, s32[1,768]{1,0:T(1,128)} %pad.8.tgt, s32[1024,2]{1,0:T(8,128)} %copy-done.3, f32[1024,2]{1,0:T(8,128)} %copy-done.4, f32[1024,2048]{1,0:T(8,128)} %shard_map.79.refs_0_, bf16[1024,2048]{1,0:T(8,128)(2,1)} %refs_1_.1, bf16[320,2048]{1,0:T(8,128)(2,1)} %copy-done.8, ...), custom_call_target="tpu_custom_call" | custom-call | flops 6442450944 | bytes 20000000 | tf_op jit(solution)/shard_map/pallas_call | solution.py:240
  (57 shorter events, 13.6 us)
Async XLA Ops:
  2.7 0.7 copy-start.2
  12.8 0.8 copy-start.3
  13.6 0.8 copy-start.4
  14.4 19.4 %copy-start.10 = (u32[8]{0:T(128)S(1)}, u32[8]{0:T(128)}, u32[]{:S(2)}) copy-start(u32[8]{0:T(128)} %constant.35) | copy-start | bytes 100
  26.0 1.1 copy-start
  27.1 1.1 copy-start.1
  28.1 125.7 %collective-permute-start = (bf16[320,2048]{1,0:T(8,128)(2,1)}, bf16[320,2048]{1,0:T(8,128)(2,1)}, u32[]{:S(2)}, u32[]{:S(2)}) collective-permute-start(bf16[320,2048]{1,0:T(8,128)(2,1)} %get-tuple-element.35), channel_id=1, source_target_pairs={{0,1},{1,0},{2,3},{3,2},{4,5},{5,4},{6,7},{7,6}} | collective-permute-start | bytes 3932168 | tf_op jit(solution)/shard_map/ppermute | solution.py:267
  28.9 176.0 %collective-permute-start.2 = (bf16[320,2048]{1,0:T(8,128)(2,1)}, bf16[320,2048]{1,0:T(8,128)(2,1)}, u32[]{:S(2)}, u32[]{:S(2)}) collective-permute-start(bf16[320,2048]{1,0:T(8,128)(2,1)} %get-tuple-element.39), channel_id=1, source_target_pairs={{0,2},{1,3},{2,0},{3,1},{4,6},{5,7},{6,4},{7,5}} | collective-permute-start | bytes 3932168 | tf_op jit(solution)/shard_map/ppermute | solution.py:267
  31.4 173.5 %collective-permute-start.3 = (bf16[320,2048]{1,0:T(8,128)(2,1)}, bf16[320,2048]{1,0:T(8,128)(2,1)}, u32[]{:S(2)}, u32[]{:S(2)}) collective-permute-start(bf16[320,2048]{1,0:T(8,128)(2,1)} %get-tuple-element.40), channel_id=1, source_target_pairs={{0,3},{1,2},{2,1},{3,0},{4,7},{5,6},{6,5},{7,4}} | collective-permute-start | bytes 3932168 | tf_op jit(solution)/shard_map/ppermute | solution.py:267
  31.5 220.3 %collective-permute-start.4 = (bf16[320,2048]{1,0:T(8,128)(2,1)}, bf16[320,2048]{1,0:T(8,128)(2,1)}, u32[]{:S(2)}, u32[]{:S(2)}) collective-permute-start(bf16[320,2048]{1,0:T(8,128)(2,1)} %get-tuple-element.43), channel_id=1, source_target_pairs={{0,2},{1,3},{2,0},{3,1},{4,6},{5,7},{6,4},{7,5}} | collective-permute-start | bytes 3932168 | tf_op jit(solution)/shard_map/ppermute | solution.py:267
  33.3 218.6 %collective-permute-start.5 = (bf16[320,2048]{1,0:T(8,128)(2,1)}, bf16[320,2048]{1,0:T(8,128)(2,1)}, u32[]{:S(2)}, u32[]{:S(2)}) collective-permute-start(bf16[320,2048]{1,0:T(8,128)(2,1)} %get-tuple-element.44), channel_id=1, source_target_pairs={{0,3},{1,2},{2,1},{3,0},{4,7},{5,6},{6,5},{7,4}} | collective-permute-start | bytes 3932168 | tf_op jit(solution)/shard_map/ppermute | solution.py:267
  153.8 149.4 %collective-permute-start.6 = (bf16[320,2048]{1,0:T(8,128)(2,1)S(1)}, bf16[320,2048]{1,0:T(8,128)(2,1)S(1)}, u32[]{:S(2)}, u32[]{:S(2)}) collective-permute-start(bf16[320,2048]{1,0:T(8,128)(2,1)S(1)} %get-tuple-element.48), channel_id=1, source_target_pairs={{0,1},{1,0},{2,3},{3,2},{4,5},{5,4},{6,7},{7,6}} | collective-permute-start | bytes 3932168 | tf_op jit(solution)/shard_map/ppermute | solution.py:267
  303.3 1.1 copy-start.5
  304.3 49.2 %copy-start.6 = (bf16[320,2048]{1,0:T(8,128)(2,1)S(1)}, bf16[320,2048]{1,0:T(8,128)(2,1)}, u32[]{:S(2)}) copy-start(bf16[320,2048]{1,0:T(8,128)(2,1)} %get-tuple-element.37) | copy-start | bytes 3932164
  304.3 57.6 %copy-start.7 = (bf16[320,2048]{1,0:T(8,128)(2,1)S(1)}, bf16[320,2048]{1,0:T(8,128)(2,1)}, u32[]{:S(2)}) copy-start(bf16[320,2048]{1,0:T(8,128)(2,1)} %get-tuple-element.52) | copy-start | bytes 3932164
  351.6 10.3 %collective-permute-start.7 = (bf16[320,2048]{1,0:T(8,128)(2,1)}, bf16[320,2048]{1,0:T(8,128)(2,1)}, u32[]{:S(2)}, u32[]{:S(2)}) collective-permute-start(bf16[320,2048]{1,0:T(8,128)(2,1)} %get-tuple-element.50), channel_id=1, source_target_pairs={{0,1},{1,0},{2,3},{3,2},{4,5},{5,4},{6,7},{7,6}} | collective-permute-start | bytes 3932168 | tf_op jit(solution)/shard_map/ppermute | solution.py:267
  351.6 32.0 %collective-permute-start.8 = (bf16[320,2048]{1,0:T(8,128)(2,1)}, bf16[320,2048]{1,0:T(8,128)(2,1)}, u32[]{:S(2)}, u32[]{:S(2)}) collective-permute-start(bf16[320,2048]{1,0:T(8,128)(2,1)} %get-tuple-element.41), channel_id=1, source_target_pairs={{0,2},{1,3},{2,0},{3,1},{4,6},{5,7},{6,4},{7,5}} | collective-permute-start | bytes 3932168 | tf_op jit(solution)/shard_map/ppermute | solution.py:267
  351.7 59.0 %collective-permute-start.9 = (bf16[320,2048]{1,0:T(8,128)(2,1)}, bf16[320,2048]{1,0:T(8,128)(2,1)}, u32[]{:S(2)}, u32[]{:S(2)}) collective-permute-start(bf16[320,2048]{1,0:T(8,128)(2,1)} %get-tuple-element.51), channel_id=1, source_target_pairs={{0,3},{1,2},{2,1},{3,0},{4,7},{5,6},{6,5},{7,4}} | collective-permute-start | bytes 3932168 | tf_op jit(solution)/shard_map/ppermute | solution.py:267
  353.5 57.2 %collective-permute-start.1 = (bf16[320,2048]{1,0:T(8,128)(2,1)S(1)}, bf16[320,2048]{1,0:T(8,128)(2,1)}, u32[]{:S(2)}, u32[]{:S(2)}) collective-permute-start(bf16[320,2048]{1,0:T(8,128)(2,1)S(1)} %copy-done.6), channel_id=1, source_target_pairs={{0,1},{1,0},{2,3},{3,2},{4,5},{5,4},{6,7},{7,6}} | collective-permute-start | bytes 3932168 | tf_op jit(solution)/shard_map/ppermute | solution.py:267
  361.8 77.9 %collective-permute-start.10 = (bf16[320,2048]{1,0:T(8,128)(2,1)}, bf16[320,2048]{1,0:T(8,128)(2,1)S(1)}, u32[]{:S(2)}, u32[]{:S(2)}) collective-permute-start(bf16[320,2048]{1,0:T(8,128)(2,1)} %get-tuple-element.45), channel_id=1, source_target_pairs={{0,2},{1,3},{2,0},{3,1},{4,6},{5,7},{6,4},{7,5}} | collective-permute-start | bytes 3932168 | tf_op jit(solution)/shard_map/ppermute | solution.py:267
  361.9 104.9 %collective-permute-start.11 = (bf16[320,2048]{1,0:T(8,128)(2,1)S(1)}, bf16[320,2048]{1,0:T(8,128)(2,1)S(1)}, u32[]{:S(2)}, u32[]{:S(2)}) collective-permute-start(bf16[320,2048]{1,0:T(8,128)(2,1)S(1)} %copy-done.7), channel_id=1, source_target_pairs={{0,3},{1,2},{2,1},{3,0},{4,7},{5,6},{6,5},{7,4}} | collective-permute-start | bytes 3932168 | tf_op jit(solution)/shard_map/ppermute | solution.py:267
  439.7 27.1 %copy-start.8 = (bf16[320,2048]{1,0:T(8,128)(2,1)}, bf16[320,2048]{1,0:T(8,128)(2,1)S(1)}, u32[]{:S(2)}) copy-start(bf16[320,2048]{1,0:T(8,128)(2,1)S(1)} %collective-permute-done.10.refs_2_) | copy-start | bytes 3932164
  466.8 1.1 copy-start.9
